TPU v7x, 32 devices: a whole 2x2x4 slice. The times are simulated.
32 devices in a mesh: seq: 8 (over z, x), head: 4 (over y, core).
Axes of the slice: x: 2, y: 2, z: 4, core: 2. Of those that a mesh axis runs over, the one named last changes fastest.
Arguments:
- context: bfloat16 [4, 4096, 1024], P('head', 'seq'), may hold values from -6 to 6
- latents: bfloat16 [4, 1024, 1024], P('head'), may hold values from -6 to 6
- offsets: int32 [4], P('head'), may hold values from 0 to 3072
- query_gain: float32 [1024], replicated, may hold values from 0.1 to 1.9
- key_gain: float32 [1024], replicated, may hold values from 0.1 to 1.9
- layer_gain: float32 [2, 1024], replicated, may hold values from 0.1 to 1.9
- cross_query: bfloat16 [1024, 1024], P(('seq', 'head')), may hold values from -0.25 to 0.25
- cross_key: bfloat16 [1024, 1024], P(('seq', 'head')), may hold values from -0.25 to 0.25
- cross_value: bfloat16 [1024, 1024], P(('seq', 'head')), may hold values from -0.1875 to 0.1875
- cross_out: bfloat16 [1024, 1024], P(('seq', 'head')), may hold values from -0.1875 to 0.1875
- layer_qkv: bfloat16 [2, 1024, 3072], P(None, ('seq', 'head')), may hold values from -0.25 to 0.25
- layer_out: bfloat16 [2, 1024, 1024], P(None, ('seq', 'head')), may hold values from -0.1875 to 0.1875
Outputs:
- latent_out: bfloat16 [4, 1024, 1024], P('head', 'seq')
Inputs may be any that keep to these rules, and one draw needn't show every extreme that they name: Latent i of row b stands at context position offsets[b] + i.
All inputs are finite; a program needn't handle non-finite values.
Results may differ from a plain program's by a relative error of at most 0.013.
Values may be sent and summed in bfloat16 or wider, within the bound.
No kernel may reach another device: no remote copies, remote signals or barrier semaphores. Data moves between devices by JAX's collectives and lax.ppermute only.
A program may use at most 128 MiB of HBM per device.

v0:
```python
import jax
import jax.numpy as jnp
from jax import lax
from jax.sharding import PartitionSpec as P

H = 16
EPSILON = 1e-06
NEGATIVE = -1e30


def rms_norm(value_matrix, gain):
    value_matrix = value_matrix.astype(jnp.float32)
    scale = lax.rsqrt(jnp.mean(value_matrix * value_matrix, axis=-1, keepdims=True) + EPSILON)
    return (value_matrix * scale * gain).astype(jnp.bfloat16)


def project(left, weight):
    return jnp.einsum("...k,kn->...n", left, weight, preferred_element_type=jnp.float32)


def block_scores(query_row_block, key_rows, query_pos, key_base, start, key_span, scale):
    key_tile = lax.dynamic_slice_in_dim(key_rows, start, key_span, 0)
    score_matrix = (
        jnp.einsum("oqi,cqi->qoc", query_row_block, key_tile, preferred_element_type=jnp.float32)
        * scale
    )
    key_pos = key_base + start + jnp.arange(key_span, dtype=jnp.int32)
    valid = key_pos[None, None, :] <= query_pos[None, :, None]
    return (jnp.where(valid, score_matrix, NEGATIVE), valid)


def causal_top(query_row_block, key_rows, query_pos, key_base, key_span, scale):

    def advance(index, best):
        start = index * key_span

        def compute(kept):
            score_matrix, valid = block_scores(
                query_row_block, key_rows, query_pos, key_base, start, key_span, scale
            )
            return jnp.maximum(kept, jnp.max(score_matrix, axis=2))

        result = compute(best)
        return result

    initial = jnp.full((query_row_block.shape[1], query_row_block.shape[0]), NEGATIVE, jnp.float32)
    return lax.fori_loop(0, key_rows.shape[0] // key_span, advance, initial)


def causal_sums(
    query_row_block, key_rows, value_rows, row_top, query_pos, key_base, key_span, scale
):

    def advance(index, carry):
        start = index * key_span

        def compute(kept):
            numerator_sum, denom = kept
            score_matrix, valid = block_scores(
                query_row_block, key_rows, query_pos, key_base, start, key_span, scale
            )
            probability_rows = jnp.where(
                valid, jnp.exp(score_matrix - row_top[:, :, None]), 0.0
            ).astype(jnp.bfloat16)
            value_tile = lax.dynamic_slice_in_dim(value_rows, start, key_span, 0)
            numerator_sum = numerator_sum + jnp.einsum(
                "ycv,vys->cys", probability_rows, value_tile, preferred_element_type=jnp.float32
            )
            denom = denom + jnp.transpose(jnp.sum(probability_rows.astype(jnp.float32), axis=2))
            return (numerator_sum, denom)

        result = compute(carry)
        return result

    count, heads, head_width = query_row_block.shape
    initial = (
        jnp.zeros((count, heads, head_width), jnp.float32),
        jnp.zeros((count, heads), jnp.float32),
    )
    return lax.fori_loop(0, key_rows.shape[0] // key_span, advance, initial)


def latent_attention(piece):
    count = piece.shape[1]
    head_width = piece.shape[-1]
    query_matrix = piece[:, :, 0]
    key_matrix = piece[:, :, 1]
    value_matrix = piece[:, :, 2]
    score_matrix = jnp.einsum(
        "bmhd,bkhd->bhmk", query_matrix, key_matrix, preferred_element_type=jnp.float32
    ) * head_width ** (-0.5)
    positions = jnp.arange(count, dtype=jnp.int32)
    valid = positions[None, :] <= positions[:, None]
    score_matrix = jnp.where(valid, score_matrix, NEGATIVE)
    row_top = jnp.max(score_matrix, axis=3, keepdims=True)
    probability_rows = jnp.where(valid, jnp.exp(score_matrix - row_top), 0.0).astype(jnp.bfloat16)
    denom = jnp.sum(probability_rows.astype(jnp.float32), axis=3)
    numerator_sum = jnp.einsum(
        "bhmk,bkhd->bmhd", probability_rows, value_matrix, preferred_element_type=jnp.float32
    )
    return (numerator_sum / jnp.transpose(denom, (0, 2, 1))[:, :, :, None]).astype(jnp.bfloat16)


def per_device(
    context,
    latents,
    offsets,
    query_gain,
    key_gain,
    layer_gain,
    cross_query,
    cross_key,
    cross_value,
    cross_out,
    layer_qkv,
    layer_out,
):
    batch, ctx_len, width = context.shape
    latent_count = latents.shape[1]
    heads = H
    head_width = width // heads
    groups = lax.axis_size("seq")
    local_rows = latent_count // groups
    group_heads = heads // groups
    seq_index = lax.axis_index("seq")
    scale = head_width ** (-0.5)
    gathered = (
        lax.all_gather(cross_query, ("seq", "head"), axis=0, tiled=True),
        lax.all_gather(cross_key, ("seq", "head"), axis=0, tiled=True),
        lax.all_gather(cross_value, ("seq", "head"), axis=0, tiled=True),
        lax.all_gather(cross_out, ("seq", "head"), axis=0, tiled=True),
        lax.all_gather(layer_qkv, ("seq", "head"), axis=1, tiled=True),
        lax.all_gather(layer_out, ("seq", "head"), axis=1, tiled=True),
    )
    normed_latents = rms_norm(latents, query_gain)
    query_matrix = project(normed_latents, gathered[0])
    query_matrix = query_matrix.astype(jnp.bfloat16)
    normed_context = rms_norm(context, key_gain)
    key_matrix = project(normed_context, gathered[1])
    value_matrix = project(normed_context, gathered[2])
    key_matrix = key_matrix.astype(jnp.bfloat16).reshape(batch, ctx_len, heads, head_width)
    value_matrix = value_matrix.astype(jnp.bfloat16).reshape(batch, ctx_len, heads, head_width)
    query_head_rows = query_matrix.reshape(batch, latent_count, heads, head_width)
    query_pos = offsets[:, None] + jnp.arange(latent_count, dtype=jnp.int32)[None, :]
    key_groups, value_groups = (
        lax.all_to_all(key_matrix, "seq", split_axis=2, concat_axis=1, tiled=True),
        lax.all_to_all(value_matrix, "seq", split_axis=2, concat_axis=1, tiled=True),
    )
    query_groups = lax.dynamic_slice_in_dim(
        query_head_rows, seq_index * group_heads, group_heads, 2
    )
    total_len = key_groups.shape[1]
    key_span = max(min(total_len, 512), total_len // 16)
    row_top = causal_top(query_groups[0], key_groups[0], query_pos[0], 0, key_span, scale)
    numerator_sum, denom = causal_sums(
        query_groups[0], key_groups[0], value_groups[0], row_top, query_pos[0], 0, key_span, scale
    )
    results = [(numerator_sum / denom[:, :, None]).astype(jnp.bfloat16)]
    attended = lax.all_to_all(
        jnp.stack(results), "seq", split_axis=1, concat_axis=2, tiled=True
    ).reshape(batch, local_rows, width)
    latents_own = lax.dynamic_slice_in_dim(latents, seq_index * local_rows, local_rows, 1)
    update = project(attended, gathered[3])
    hidden = (latents_own.astype(jnp.float32) + update).astype(jnp.bfloat16)
    for layer in range(layer_qkv.shape[0]):
        normed = rms_norm(hidden, layer_gain[layer])
        qkv = project(normed, gathered[4][layer])
        grouped = qkv.astype(jnp.bfloat16).reshape(batch, local_rows, 3, heads, head_width)
        mixed = latent_attention(
            lax.all_to_all(grouped, "seq", split_axis=3, concat_axis=1, tiled=True)
        )
        merged = lax.all_to_all(mixed, "seq", split_axis=1, concat_axis=2, tiled=True).reshape(
            batch, local_rows, width
        )
        update = project(merged, gathered[5][layer])
        hidden = (hidden.astype(jnp.float32) + update).astype(jnp.bfloat16)
    return hidden


def solution(mesh):
    return jax.shard_map(
        per_device,
        mesh=mesh,
        in_specs=(
            P("head", "seq", None),
            P("head", None, None),
            P("head"),
            P(),
            P(),
            P(),
            P(("seq", "head"), None),
            P(("seq", "head"), None),
            P(("seq", "head"), None),
            P(("seq", "head"), None),
            P(None, ("seq", "head"), None),
            P(None, ("seq", "head"), None),
        ),
        out_specs=P("head", "seq", None),
        check_vma=False,
    )
```

profile of v0, /device:TPU:0, one launch (start us, length us, event | category | flops | bytes accessed | tf_op | source)
XLA Modules:
  0.0 485.0 jit_solution(4928080488201104973)
XLA Ops:
  11.4 57.8 %all-gather.9.cloned.1.call-done = bf16[1024,1024]{1,0:T(8,128)(2,1)} async-done(((bf16[32,1024]{1,0:T(8,128)(2,1)}), bf16[1024,1024]{1,0:T(8,128)(2,1)}) %all-gather.9.cloned.1.call-update) | async-done | bytes 2097168 | tf_op jit(solution)/shard_map/all_gather | solution.py:129
  69.2 3.2 convolution_convert_fusion
  73.8 4.3 all-to-all-start.1
  80.8 51.9 %all-gather.7.cloned.1.call-done = bf16[1024,1024]{1,0:T(8,128)(2,1)} async-done(((bf16[32,1024]{1,0:T(8,128)(2,1)}), bf16[1024,1024]{1,0:T(8,128)(2,1)}) %all-gather.7.cloned.1.call-update) | async-done | bytes 2097168 | tf_op jit(solution)/shard_map/all_gather | solution.py:130
  132.7 3.9 convolution_convert_fusion.1
  138.9 51.8 %all-gather.11.cloned.1.call-done = bf16[1024,1024]{1,0:T(8,128)(2,1)} async-done(((bf16[32,1024]{1,0:T(8,128)(2,1)}), bf16[1024,1024]{1,0:T(8,128)(2,1)}) %all-gather.11.cloned.1.call-update) | async-done | bytes 2097168 | tf_op jit(solution)/shard_map/all_gather | solution.py:128
  190.7 4.8 fusion.43
  195.5 4.3 all-to-all-start
  203.0 16.9 %while.30 = (s32[]{:T(128)}, f32[2,1024]{1,0:T(2,128)S(1)}, bf16[4096,2,64]{0,2,1:T(8,128)(2,1)S(1)}, bf16[1024,2,64]{0,2,1:T(8,128)(2,1)S(1)}, s32[]{:T(128)}, ...) while((s32[]{:T(128)}, f32[2,1024]{1,0:T(2,128)S(1)}, bf16[4096,2,64]{0,2,1:T(8,128)(2,1)S(1)}, ...), condition=%wide.region_4.5_spmd.clone, body=%wide.region_2.4_spmd.clone.sunk | while | flops 137891328 | bytes 1487009 | solution.py:47
  219.9 8.5 %all-to-all-done = bf16[1,512,16,64]{1,3,0,2:T(8,128)(2,1)S(1)} async-done(((bf16[1,512,16,64]{1,3,0,2:T(8,128)(2,1)}), bf16[1,512,16,64]{1,3,0,2:T(8,128)(2,1)S(1)}, u32[]{:S(2)}, u32[]{:S(2)}) %all-to-all-start) | async-done | bytes 1048608 | tf_op jit(solution)/shard_map/all_to_all | solution.py:147
  230.2 40.6 %while.31 = (s32[]{:T(128)}, f32[1024,2,64]{0,2,1:T(8,128)S(1)}, f32[1024,2]{0,1:T(2,128)S(1)}, bf16[4096,2,64]{0,2,1:T(8,128)(2,1)}, bf16[4096,2,64]{0,2,1:T(8,...) while((s32[]{:T(128)}, f32[1024,2,64]{0,2,1:T(8,128)S(1)}, ...), condition=%wide.region_7.8_spmd.clone, body=%wide.region_5.7_spmd.clone.sunk | while | flops 276565504 | bytes 6869182 | solution.py:80
  231.3 2.5 convert_reduce_fusion.4
  236.3 2.5 convert_reduce_fusion.4
  241.5 2.5 convert_reduce_fusion.4
  251.6 2.5 convert_reduce_fusion.4
  256.7 2.5 convert_reduce_fusion.4
  272.7 3.5 all-to-all-start.2
  276.3 9.1 %all-to-all-done.2 = bf16[8,2,8192]{2,1,0:T(2,128)(2,1)S(1)} async-done(((bf16[8,2,8192]{2,1,0:T(2,128)(2,1)}), bf16[8,2,8192]{2,1,0:T(2,128)(2,1)S(1)}, u32[]{:S(2)}, u32[]{:S(2)}) %all-to-all-start.2) | async-done | bytes 262176 | tf_op jit(solution)/shard_map/all_to_all | solution.py:159
  288.3 64.0 %all-gather.15.cloned.1.call-done = bf16[2,1024,3072]{2,1,0:T(8,128)(2,1)} async-done(((bf16[2,32,3072]{2,1,0:T(8,128)(2,1)}), bf16[2,1024,3072]{2,1,0:T(8,128)(2,1)}) %all-gather.15.cloned.1.call-update) | async-done | bytes 12582928 | tf_op jit(solution)/shard_map/all_gather | solution.py:132
  352.3 3.8 fusion.31
  357.4 4.0 all-to-all-start.3
  361.8 23.0 %all-to-all-done.3 = bf16[1,128,3,16,64]{1,4,2,0,3:T(8,128)(2,1)S(1)} async-done(((bf16[1,128,3,16,64]{1,4,2,0,3:T(8,128)(2,1)}), bf16[1,128,3,16,64]{1,4,2,0,3:T(8,128)(2,1)S(1)}, u32[]{:S(2)}, u32[]{:S(2)}) %all-to-all-start.3) | async-done | bytes 786464 | tf_op jit(solution)/shard_map/all_to_all | solution.py:170
  385.6 6.0 %convert_reduce_fusion.2 = (f32[2,1024]{1,0:T(2,128)S(1)}, bf16[2,1024,1024]{1,2,0:T(8,128)(2,1)}) fusion(pred[1024,1024]{0,1:T(8,128)(4,1)S(1)} %iota_compare_fusion, bf16[1,1024,3,2,64]{1,4,3,2,0:T(8,128)(2,1)S(1)} %all_to_all.93), kind=kOutput, calls=%fused_computation.31 | convolution fusion | flops 283116544 | bytes 6823936 | tf_op jit(solution)/shard_map/sub | solution.py:96
  391.6 3.0 fusion.57
  395.5 18.1 %all_to_all.111 = bf16[8,2,8192]{2,1,0:T(2,128)(2,1)S(1)} all-to-all(bf16[8,2,8192]{2,1,0:T(2,128)(2,1)S(1)} %reshape.309), channel_id=1, replica_groups=mesh['seq'=8,'head'=4] {'seq'}, dimensions={0} | all-to-all | bytes 524288 | tf_op jit(solution)/shard_map/all_to_all | solution.py:172
  414.2 6.9 %all-gather.17.cloned.1.call-done = bf16[2,1024,1024]{2,1,0:T(8,128)(2,1)} async-done(((bf16[2,32,1024]{2,1,0:T(8,128)(2,1)}), bf16[2,1024,1024]{2,1,0:T(8,128)(2,1)}) %all-gather.17.cloned.1.call-update) | async-done | bytes 4194320 | tf_op jit(solution)/shard_map/all_gather | solution.py:133
  423.3 3.8 fusion.32
  427.6 24.1 %all_to_all.112 = bf16[1,128,3,16,64]{1,4,2,0,3:T(8,128)(2,1)S(1)} all-to-all(bf16[1,128,3,16,64]{1,4,2,0,3:T(8,128)(2,1)S(1)} %copy.89), channel_id=1, replica_groups=mesh['seq'=8,'head'=4] {'seq'}, dimensions={3} | all-to-all | bytes 1572864 | tf_op jit(solution)/shard_map/all_to_all | solution.py:170
  452.5 6.0 %convert_reduce_fusion.1 = (f32[2,1024]{1,0:T(2,128)S(1)}, bf16[2,1024,1024]{1,2,0:T(8,128)(2,1)}) fusion(pred[1024,1024]{0,1:T(8,128)(4,1)S(1)} %iota_compare_fusion, bf16[1,1024,3,2,64]{1,4,3,2,0:T(8,128)(2,1)S(1)} %all_to_all.100), kind=kOutput, calls=%fused_computation.28 | convolution fusion | flops 283116544 | bytes 6823936 | tf_op jit(solution)/shard_map/sub | solution.py:96
  458.5 3.0 fusion.59
  462.4 12.3 %all_to_all.113 = bf16[8,2,8192]{2,1,0:T(2,128)(2,1)S(1)} all-to-all(bf16[8,2,8192]{2,1,0:T(2,128)(2,1)S(1)} %reshape.311), channel_id=1, replica_groups=mesh['seq'=8,'head'=4] {'seq'}, dimensions={0} | all-to-all | bytes 524288 | tf_op jit(solution)/shard_map/all_to_all | solution.py:172
  475.4 2.8 fusion.55
  (152 shorter events, 73.6 us)
Async XLA Ops:
  6.5 62.7 %all-gather.9.cloned.1.call-start = ((), (), s32[]{:S(2)}) async-start(), calls=%async_computation.8 | async-start | bytes 2162688 | tf_op jit(solution)/shard_map/all_gather | solution.py:129
  7.3 125.4 %all-gather.7.cloned.1.call-start = ((), (), s32[]{:S(2)}) async-start(), calls=%async_computation.7 | async-start | bytes 2162688 | tf_op jit(solution)/shard_map/all_gather | solution.py:130
  8.0 182.7 %all-gather.11.cloned.1.call-start = ((), (), s32[]{:S(2)}) async-start(), calls=%async_computation.9 | async-start | bytes 2162688 | tf_op jit(solution)/shard_map/all_gather | solution.py:128
  8.7 277.4 %all-gather.13.cloned.1.call-start = ((), (), s32[]{:S(2)}) async-start(), calls=%async_computation.10 | async-start | bytes 2162688 | tf_op jit(solution)/shard_map/all_gather | solution.py:131
  9.3 343.0 %all-gather.15.cloned.1.call-start = ((), (), s32[]{:S(2)}) async-start(), calls=%async_computation.11 | async-start | bytes 12976128 | tf_op jit(solution)/shard_map/all_gather | solution.py:132
  72.4 60.3 %copy-start = (bf16[1,512,1024]{2,1,0:T(8,128)(2,1)S(1)}, bf16[1,512,1024]{2,1,0:T(8,128)(2,1)}, u32[]{:S(2)}) copy-start(bf16[1,512,1024]{2,1,0:T(8,128)(2,1)} %param.16) | copy-start | bytes 3145732
  72.4 60.2 %copy-start.3 = (f32[1024]{0:T(1024)S(1)}, f32[1024]{0:T(1024)}, u32[]{:S(2)}) copy-start(f32[1024]{0:T(1024)} %param.20) | copy-start | bytes 12292
  73.8 121.7 %all-to-all-start.1 = ((bf16[1,512,16,64]{1,3,0,2:T(8,128)(2,1)}), bf16[1,512,16,64]{1,3,0,2:T(8,128)(2,1)S(1)}, u32[]{:S(2)}, u32[]{:S(2)}) async-start(bf16[1,512,16,64]{1,3,0,2:T(8,128)(2,1)} %bitcast.6), calls=%async_computation.1 | async-start | bytes 2097152 | tf_op jit(solution)/shard_map/all_to_all | solution.py:146
  78.1 343.1 %all-gather.17.cloned.1.call-start = ((), (), s32[]{:S(2)}) async-start(), calls=%async_computation.12 | async-start | bytes 4325376 | tf_op jit(solution)/shard_map/all_gather | solution.py:133
  80.8 109.9 %copy-start.4 = (f32[1024]{0:T(1024)S(1)}, f32[1024]{0:T(1024)}, u32[]{:S(2)}) copy-start(f32[1024]{0:T(1024)} %param.19) | copy-start | bytes 12292
  195.5 32.8 %all-to-all-start = ((bf16[1,512,16,64]{1,3,0,2:T(8,128)(2,1)}), bf16[1,512,16,64]{1,3,0,2:T(8,128)(2,1)S(1)}, u32[]{:S(2)}, u32[]{:S(2)}) async-start(bf16[1,512,16,64]{1,3,0,2:T(8,128)(2,1)} %bitcast.2), calls=%async_computation | async-start | bytes 2097152 | tf_op jit(solution)/shard_map/all_to_all | solution.py:147
  219.8 8.5 %copy-start.1 = (bf16[4096,2,64]{0,2,1:T(8,128)(2,1)}, bf16[4096,2,64]{0,2,1:T(8,128)(2,1)S(1)}, u32[]{:S(2)}) copy-start(bf16[4096,2,64]{0,2,1:T(8,128)(2,1)S(1)} %get-tuple-element.490) | copy-start | bytes 3145732
  230.2 46.0 %copy-start.2 = (f32[2,1024]{1,0:T(2,128)S(1)}, f32[2,1024]{1,0:T(2,128)}, u32[]{:S(2)}) copy-start(f32[2,1024]{1,0:T(2,128)} %param.21) | copy-start | bytes 24580
  272.7 12.7 %all-to-all-start.2 = ((bf16[8,2,8192]{2,1,0:T(2,128)(2,1)}), bf16[8,2,8192]{2,1,0:T(2,128)(2,1)S(1)}, u32[]{:S(2)}, u32[]{:S(2)}) async-start(bf16[8,2,8192]{2,1,0:T(2,128)(2,1)} %reshape.307), calls=%async_computation.2 | async-start | bytes 524288 | tf_op jit(solution)/shard_map/all_to_all | solution.py:159
  357.4 27.3 %all-to-all-start.3 = ((bf16[1,128,3,16,64]{1,4,2,0,3:T(8,128)(2,1)}), bf16[1,128,3,16,64]{1,4,2,0,3:T(8,128)(2,1)S(1)}, u32[]{:S(2)}, u32[]{:S(2)}) async-start(bf16[1,128,3,16,64]{1,4,2,0,3:T(8,128)(2,1)} %copy.82), calls=%async_computation.3 | async-start | bytes 1572864 | tf_op jit(solution)/shard_map/all_to_all | solution.py:170
Sparse Core Ops, SparseCore 0:
  10.2 58.9 all-gather.8
  72.0 60.5 all-gather.6
  135.5 55.0 all-gather.10
  193.4 61.0 all-gather.12
  257.3 94.9 all-gather.14
  355.1 66.0 all-gather.16
where the time goes:
time: 486 us; the launch traced here: 485 us
  waiting for transfers between devices  277 us (57%)
  matrix products  84.7 us (17%)
  blocking collectives  54.5 us (11%)
  other arithmetic  20.5 us (4%)
  local copies, waits for them, and re-layouts  17.5 us (4%)
  starting transfers between devices  16.4 us (3%)
  between operations  13.8 us (3%)
    all_gather x1, waiting for transfers between devices, per_device(): lax.all_gather(layer_qkv, ('seq', 'head'), axis=1, tiled=True)  64 us
    all_gather x1, waiting for transfers between devices, per_device(): lax.all_gather(cross_key, ('seq', 'head'), axis=0, tiled=True)  57.8 us
    all_gather x1, waiting for transfers between devices, per_device(): lax.all_gather(cross_value, ('seq', 'head'), axis=0, tiled=True)  51.9 us
    all_gather x1, waiting for transfers between devices, per_device(): lax.all_gather(cross_query, ('seq', 'head'), axis=0, tiled=True)  51.8 us
    all_to_all x2, blocking collectives, per_device(): lax.all_to_all(mixed, 'seq', split_axis=1, concat_axis=2, tiled=True)  30.4 us
    dot_general x16, matrix products, block_scores(): jnp.einsum('oqi,cqi->qoc', query_row_block, key_tile, preferred_element_t...  28.3 us
    dot_general x8, matrix products, project(): jnp.einsum('...k,kn->...n', left, weight, preferred_element_type=jnp.floa...  26.6 us
    all_to_all x1, blocking collectives, per_device(): lax.all_to_all(grouped, 'seq', split_axis=3, concat_axis=1, tiled=True)  24.1 us
  transfers between devices with their start and end apart: 10, of which 8 were waited for; matrix products, arithmetic and copies ran while one was open for 21% of the time, Pallas kernels for 0%

commit v1 on v0

--- a/solution.py
+++ b/solution.py
@@ -6,6 +6,13 @@
 H = 16
 EPSILON = 1e-06
 NEGATIVE = -1e30
+
+
+def swapped_in(x, name, dim):
+    devices = lax.axis_size(name)
+    blocks = jnp.stack([x for _ in range(devices)])
+    blocks = lax.all_to_all(blocks, name, split_axis=0, concat_axis=0)
+    return jnp.concatenate(blocks, axis=dim)
 
 
 def rms_norm(value_matrix, gain):
@@ -129,7 +136,7 @@
         lax.all_gather(cross_key, ("seq", "head"), axis=0, tiled=True),
         lax.all_gather(cross_value, ("seq", "head"), axis=0, tiled=True),
         lax.all_gather(cross_out, ("seq", "head"), axis=0, tiled=True),
-        lax.all_gather(layer_qkv, ("seq", "head"), axis=1, tiled=True),
+        swapped_in(layer_qkv, ("seq", "head"), 1),
         lax.all_gather(layer_out, ("seq", "head"), axis=1, tiled=True),
     )
     normed_latents = rms_norm(latents, query_gain)

time: 486 us -> 724 us (1.49)
  waiting for transfers between devices: 277 us -> 493 us
  local copies, waits for them, and re-layouts: 17.5 us -> 31.7 us
    all_to_all x1, waiting for transfers between devices: 9.13 us -> 164 us  [swapped_in(): blocks = lax.all_to_all(blocks, name, split_axis=0, concat_axis=0)]
    all_gather x1, waiting for transfers between devices: 0.02 us -> 137 us  [per_device(): lax.all_gather(cross_out, ('seq', 'head'), axis=0, tiled=True)]
    all_gather x1 -> x0, waiting for transfers between devices: 64 us -> none  [per_device(): lax.all_gather(layer_qkv, ('seq', 'head'), axis=1, tiled=True)]
    all_to_all x0 -> x1, blocking collectives: none -> 12.5 us  [per_device(): lax.all_to_all(jnp.stack(results), 'seq', split_axis=1, concat_axis=2, ti...]
    slice x0 -> x1, local copies, waits for them, and re-layouts: none -> 8.79 us  [per_device(): qkv = project(normed, gathered[4][layer])]
  transfers between devices with their start and end apart: 10 -> 9, of which waited for: 8 -> 7; matrix products, arithmetic and copies ran while one was open for 21% -> 9% of each run, Pallas kernels for 0% -> 0%
where the time goes in v1:
time: 724 us; the launch traced here: 718 us
  waiting for transfers between devices  493 us (68%)
  matrix products  83.1 us (11%)
  blocking collectives  59.1 us (8%)
  local copies, waits for them, and re-layouts  31.7 us (4%)
  other arithmetic  20.5 us (3%)
  starting transfers between devices  16.5 us (2%)
  between operations  13.5 us (2%)
    all_to_all x1, waiting for transfers between devices, swapped_in(): blocks = lax.all_to_all(blocks, name, split_axis=0, concat_axis=0)  164 us
    all_gather x1, waiting for transfers between devices, per_device(): lax.all_gather(cross_out, ('seq', 'head'), axis=0, tiled=True)  137 us
    all_gather x1, waiting for transfers between devices, per_device(): lax.all_gather(cross_key, ('seq', 'head'), axis=0, tiled=True)  58.9 us
    all_gather x1, waiting for transfers between devices, per_device(): lax.all_gather(cross_value, ('seq', 'head'), axis=0, tiled=True)  52.4 us
    all_gather x1, waiting for transfers between devices, per_device(): lax.all_gather(cross_query, ('seq', 'head'), axis=0, tiled=True)  51.8 us
    dot_general x16, matrix products, block_scores(): jnp.einsum('oqi,cqi->qoc', query_row_block, key_tile, preferred_element_t...  28.3 us
    dot_general x8, matrix products, project(): jnp.einsum('...k,kn->...n', left, weight, preferred_element_type=jnp.floa...  23.9 us
    all_to_all x2, blocking collectives, per_device(): lax.all_to_all(mixed, 'seq', split_axis=1, concat_axis=2, tiled=True)  23.6 us
  transfers between devices with their start and end apart: 9, of which 7 were waited for; matrix products, arithmetic and copies ran while one was open for 9% of the time, Pallas kernels for 0%

profile of v1, /device:TPU:0, one launch (start us, length us, event | category | flops | bytes accessed | tf_op | source)
XLA Modules:
  0.0 718.0 jit_solution(2045044767840756438)
XLA Ops:
  10.3 58.9 %all-gather.8.cloned.1.call-done = bf16[1024,1024]{1,0:T(8,128)(2,1)} async-done(((bf16[32,1024]{1,0:T(8,128)(2,1)}), bf16[1024,1024]{1,0:T(8,128)(2,1)}) %all-gather.8.cloned.1.call-update) | async-done | bytes 2097168 | tf_op jit(solution)/shard_map/all_gather | solution.py:136
  69.2 3.2 convolution_convert_fusion.2
  73.8 4.3 all-to-all-start.1
  80.2 52.4 %all-gather.6.cloned.1.call-done = bf16[1024,1024]{1,0:T(8,128)(2,1)} async-done(((bf16[32,1024]{1,0:T(8,128)(2,1)}), bf16[1024,1024]{1,0:T(8,128)(2,1)}) %all-gather.6.cloned.1.call-update) | async-done | bytes 2097168 | tf_op jit(solution)/shard_map/all_gather | solution.py:137
  132.7 3.9 convolution_convert_fusion.3
  138.8 51.8 %all-gather.10.cloned.1.call-done = bf16[1024,1024]{1,0:T(8,128)(2,1)} async-done(((bf16[32,1024]{1,0:T(8,128)(2,1)}), bf16[1024,1024]{1,0:T(8,128)(2,1)}) %all-gather.10.cloned.1.call-update) | async-done | bytes 2097168 | tf_op jit(solution)/shard_map/all_gather | solution.py:135
  190.7 4.8 fusion.39
  195.5 4.3 all-to-all-start
  202.9 16.9 %while.30 = (s32[]{:T(128)}, f32[2,1024]{1,0:T(2,128)S(1)}, bf16[4096,2,64]{0,2,1:T(8,128)(2,1)S(1)}, bf16[1024,2,64]{0,2,1:T(8,128)(2,1)S(1)}, s32[]{:T(128)}, ...) while((s32[]{:T(128)}, f32[2,1024]{1,0:T(2,128)S(1)}, bf16[4096,2,64]{0,2,1:T(8,128)(2,1)S(1)}, ...), condition=%wide.region_4.5_spmd.clone, body=%wide.region_2.4_spmd.clone.sunk | while | flops 137891328 | bytes 1487009 | solution.py:54
  219.8 6.2 all-to-all-done
  227.9 40.5 %while.31 = (s32[]{:T(128)}, f32[1024,2,64]{0,2,1:T(8,128)S(1)}, f32[1024,2]{0,1:T(2,128)S(1)}, bf16[4096,2,64]{0,2,1:T(8,128)(2,1)}, bf16[4096,2,64]{0,2,1:T(8,...) while((s32[]{:T(128)}, f32[1024,2,64]{0,2,1:T(8,128)S(1)}, ...), condition=%wide.region_7.8_spmd.clone, body=%wide.region_5.7_spmd.clone.sunk | while | flops 276565504 | bytes 6869182 | solution.py:87
  228.9 2.5 convert_reduce_fusion.4
  234.0 2.5 convert_reduce_fusion.4
  239.1 2.5 convert_reduce_fusion.4
  244.1 2.5 convert_reduce_fusion.4
  269.6 12.5 %all_to_all.116 = bf16[8,2,8192]{2,1,0:T(2,128)(2,1)S(1)} all-to-all(bf16[8,2,8192]{2,1,0:T(2,128)(2,1)S(1)} %reshape.318), channel_id=1, replica_groups=mesh['seq'=8,'head'=4] {'seq'}, dimensions={0} | all-to-all | bytes 524288 | tf_op jit(solution)/shard_map/all_to_all | solution.py:166
  282.1 6.1 stack.5
  288.2 3.9 all-to-all-start.3
  294.0 136.6 %all-gather.12.cloned.1.call-done = bf16[1024,1024]{1,0:T(8,128)(2,1)} async-done(((bf16[32,1024]{1,0:T(8,128)(2,1)}), bf16[1024,1024]{1,0:T(8,128)(2,1)}) %all-gather.12.cloned.1.call-update) | async-done | bytes 2097168 | tf_op jit(solution)/shard_map/all_gather | solution.py:138
  432.7 164.2 %all-to-all-done.3 = bf16[32,2,32,3072]{3,2,1,0:T(8,128)(2,1)} async-done(((bf16[32,2,32,3072]{3,2,1,0:T(8,128)(2,1)}), bf16[32,2,32,3072]{3,2,1,0:T(8,128)(2,1)}, u32[]{:S(2)}, u32[]{:S(2)}) %all-to-all-start.3) | async-done | bytes 12582944 | tf_op jit(solution)/shard_map/all_to_all | solution.py:14
  596.9 8.8 %fusion.77 = (bf16[1,32,32,3072]{3,2,0,1:T(8,128)(2,1)}, bf16[1,32,32,3072]{3,2,0,1:T(8,128)(2,1)S(1)}) fusion(bf16[2,32,32,3072]{3,2,0,1:T(8,128)(2,1)} %bitcast.20), kind=kLoop, calls=%fused_computation.116 | loop fusion | bytes 25165824 | tf_op jit(solution)/shard_map/slice | solution.py:174
  608.1 3.8 all-to-all-start.4
  612.2 19.5 %all-to-all-done.4 = bf16[1,128,3,16,64]{1,4,2,0,3:T(8,128)(2,1)S(1)} async-done(((bf16[1,128,3,16,64]{1,4,2,0,3:T(8,128)(2,1)}), bf16[1,128,3,16,64]{1,4,2,0,3:T(8,128)(2,1)S(1)}, u32[]{:S(2)}, u32[]{:S(2)}) %all-to-all-start.4) | async-done | bytes 786464 | tf_op jit(solution)/shard_map/all_to_all | solution.py:177
  632.5 6.0 convert_reduce_fusion.2
  638.5 3.0 fusion.53
  642.3 11.7 %all_to_all.117 = bf16[8,2,8192]{2,1,0:T(2,128)(2,1)S(1)} all-to-all(bf16[8,2,8192]{2,1,0:T(2,128)(2,1)S(1)} %reshape.320), channel_id=1, replica_groups=mesh['seq'=8,'head'=4] {'seq'}, dimensions={0} | all-to-all | bytes 524288 | tf_op jit(solution)/shard_map/all_to_all | solution.py:179
  656.9 3.8 convolution_convert_fusion
  661.2 22.9 %all_to_all.118 = bf16[1,128,3,16,64]{1,4,2,0,3:T(8,128)(2,1)S(1)} all-to-all(bf16[1,128,3,16,64]{1,4,2,0,3:T(8,128)(2,1)S(1)} %copy.89), channel_id=1, replica_groups=mesh['seq'=8,'head'=4] {'seq'}, dimensions={3} | all-to-all | bytes 1572864 | tf_op jit(solution)/shard_map/all_to_all | solution.py:177
  685.0 7.3 %convert_reduce_fusion.1 = (f32[2,1024]{1,0:T(2,128)S(1)}, bf16[2,1024,1024]{1,2,0:T(8,128)(2,1)}) fusion(pred[1024,1024]{0,1:T(8,128)(4,1)} %copy-done.2, bf16[1,1024,3,2,64]{1,4,3,2,0:T(8,128)(2,1)S(1)} %all_to_all.104), kind=kOutput, calls=%fused_computation.28 | convolution fusion | flops 283116544 | bytes 6823936 | tf_op jit(solution)/shard_map/sub | solution.py:103
  692.3 3.0 fusion.55
  696.1 11.9 %all_to_all.119 = bf16[8,2,8192]{2,1,0:T(2,128)(2,1)S(1)} all-to-all(bf16[8,2,8192]{2,1,0:T(2,128)(2,1)S(1)} %reshape.322), channel_id=1, replica_groups=mesh['seq'=8,'head'=4] {'seq'}, dimensions={0} | all-to-all | bytes 524288 | tf_op jit(solution)/shard_map/all_to_all | solution.py:179
  708.7 2.8 fusion.51
  (156 shorter events, 75.7 us)
Async XLA Ops:
  6.5 62.7 %all-gather.8.cloned.1.call-start = ((), (), s32[]{:S(2)}) async-start(), calls=%async_computation.9 | async-start | bytes 2162688 | tf_op jit(solution)/shard_map/all_gather | solution.py:136
  7.3 125.4 %all-gather.6.cloned.1.call-start = ((), (), s32[]{:S(2)}) async-start(), calls=%async_computation.8 | async-start | bytes 2162688 | tf_op jit(solution)/shard_map/all_gather | solution.py:137
  8.0 182.7 %all-gather.10.cloned.1.call-start = ((), (), s32[]{:S(2)}) async-start(), calls=%async_computation.10 | async-start | bytes 2162688 | tf_op jit(solution)/shard_map/all_gather | solution.py:135
  72.4 60.2 %copy-start = (bf16[1,512,1024]{2,1,0:T(8,128)(2,1)S(1)}, bf16[1,512,1024]{2,1,0:T(8,128)(2,1)}, u32[]{:S(2)}) copy-start(bf16[1,512,1024]{2,1,0:T(8,128)(2,1)} %param.16) | copy-start | bytes 3145732
  72.4 60.2 %copy-start.5 = (f32[1024]{0:T(1024)S(1)}, f32[1024]{0:T(1024)}, u32[]{:S(2)}) copy-start(f32[1024]{0:T(1024)} %param.20) | copy-start | bytes 12292
  73.8 121.7 %all-to-all-start.1 = ((bf16[1,512,16,64]{1,3,0,2:T(8,128)(2,1)}), bf16[1,512,16,64]{1,3,0,2:T(8,128)(2,1)S(1)}, u32[]{:S(2)}, u32[]{:S(2)}) async-start(bf16[1,512,16,64]{1,3,0,2:T(8,128)(2,1)} %bitcast.6), calls=%async_computation.1 | async-start | bytes 2097152 | tf_op jit(solution)/shard_map/all_to_all | solution.py:153
  80.2 110.4 %copy-start.6 = (f32[1024]{0:T(1024)S(1)}, f32[1024]{0:T(1024)}, u32[]{:S(2)}) copy-start(f32[1024]{0:T(1024)} %param.19) | copy-start | bytes 12292
  195.5 30.5 %all-to-all-start = ((bf16[1,512,16,64]{1,3,0,2:T(8,128)(2,1)}), bf16[1,512,16,64]{1,3,0,2:T(8,128)(2,1)S(1)}, u32[]{:S(2)}, u32[]{:S(2)}) async-start(bf16[1,512,16,64]{1,3,0,2:T(8,128)(2,1)} %bitcast.2), calls=%async_computation | async-start | bytes 2097152 | tf_op jit(solution)/shard_map/all_to_all | solution.py:154
  219.8 6.2 copy-start.1
  268.4 13.8 %copy-start.3 = (bf16[2,32,3072]{2,1,0:T(8,128)(2,1)S(1)}, bf16[2,32,3072]{2,1,0:T(8,128)(2,1)}, u32[]{:S(2)}) copy-start(bf16[2,32,3072]{2,1,0:T(8,128)(2,1)} %param.26) | copy-start | bytes 1179652
  288.2 5.1 copy-start.4
  288.2 308.7 %all-to-all-start.3 = ((bf16[32,2,32,3072]{3,2,1,0:T(8,128)(2,1)}), bf16[32,2,32,3072]{3,2,1,0:T(8,128)(2,1)}, u32[]{:S(2)}, u32[]{:S(2)}) async-start(bf16[32,2,32,3072]{3,2,1,0:T(8,128)(2,1)} %stack.5), calls=%async_computation.3 | async-start | bytes 25165824 | tf_op jit(solution)/shard_map/all_to_all | solution.py:14
  292.1 138.5 %all-gather.12.cloned.1.call-start = ((), (), s32[]{:S(2)}) async-start(), calls=%async_computation.11 | async-start | bytes 2162688 | tf_op jit(solution)/shard_map/all_gather | solution.py:138
  292.7 362.1 %all-gather.14.cloned.1.call-start = ((), (), s32[]{:S(2)}) async-start(), calls=%async_computation.12 | async-start | bytes 4325376 | tf_op jit(solution)/shard_map/all_gather | solution.py:140
  608.1 23.6 %all-to-all-start.4 = ((bf16[1,128,3,16,64]{1,4,2,0,3:T(8,128)(2,1)}), bf16[1,128,3,16,64]{1,4,2,0,3:T(8,128)(2,1)S(1)}, u32[]{:S(2)}, u32[]{:S(2)}) async-start(bf16[1,128,3,16,64]{1,4,2,0,3:T(8,128)(2,1)} %copy.82), calls=%async_computation.4 | async-start | bytes 1572864 | tf_op jit(solution)/shard_map/all_to_all | solution.py:177
  612.1 26.4 %copy-start.2 = (pred[1024,1024]{0,1:T(8,128)(4,1)}, pred[1024,1024]{0,1:T(8,128)(4,1)S(1)}, u32[]{:S(2)}) copy-start(pred[1024,1024]{0,1:T(8,128)(4,1)S(1)} %iota_compare_fusion) | copy-start | bytes 3145732
Sparse Core Ops, SparseCore 0:
  10.2 58.9 all-gather.7
  72.0 60.5 all-gather.5
  135.5 55.0 all-gather.9
  295.5 135.0 all-gather.11
  433.3 112.8 all-gather.13
